TPU v7x, 128 devices: a whole 4x4x4 slice. The times are simulated.
128 devices in a mesh: row: 8 (over z, core), col: 16 (over y, x).
Axes of the slice: x: 4, y: 4, z: 4, core: 2. Of those that a mesh axis runs over, the one named last changes fastest.
Arguments:
- a_matrix: bfloat16 [16384, 16384], P('row', 'col'), may hold values from -6 to 6
- a_flags: int32 [128, 128], P('row', 'col'), may hold values from 0 to 1, as said below
- b_matrix: bfloat16 [16384, 32768], P('row', 'col'), may hold values from -0.1875 to 0.1875
- b_flags: int32 [128, 256], P('row', 'col'), may hold values from 0 to 1, as said below
- sections: int32 [2], replicated, may hold values from 0 to 15
Outputs:
- packed: bfloat16 [16384, 32768], P('row', 'col')
- tile_place: int32 [128, 256], P('row', 'col')
Inputs may be any that keep to these rules, and one draw needn't show every extreme that they name: `a_flags`: 0 or 1; the 16 x 8 tiles of one device hold at most 64 ones, and some device holds exactly 64. `b_flags`: 0 or 1; each aligned block of 8 x 16 tiles holds at most 64 ones, and some block exactly 64.
All inputs are finite; a program needn't handle non-finite values.
Results may differ from a plain program's by a relative error of at most 0.001.
Values may be sent and summed in bfloat16 or wider, within the bound.
A program may use at most 128 MiB of HBM per device.

v0:
```python
import jax
import jax.numpy as jnp
from jax import lax
from jax.sharding import PartitionSpec as P

TILE = 128
SECTIONS = 2


def spread(value, axis, source):
    kept = jnp.where(lax.axis_index(axis) == source, value, 0).astype(value.dtype)
    return lax.psum(kept, axis)


def filled_up(lines, length):
    spare = -lines.shape[0] % length
    if not spare:
        return lines
    return jnp.concatenate([lines, jnp.zeros((spare, *lines.shape[1:]), lines.dtype)])


def broadcast_by_parts(value, axis, root):
    lines = jnp.where(lax.axis_index(axis) == root, value, jnp.zeros_like(value)).reshape(
        -1, *value.shape[1:][-1:]
    )
    padded = filled_up(lines, lax.axis_size(axis))
    own = lax.psum_scatter(padded, axis, scatter_dimension=0, tiled=True)
    return lax.all_gather(own, axis, axis=0, tiled=True)[: len(lines)].reshape(value.shape)


def from_everyone(value, axis):
    copies = jnp.broadcast_to(value, (lax.axis_size(axis), *value.shape))
    return lax.all_to_all(copies, axis, split_axis=0, concat_axis=0, tiled=True)


def joined_by_halves(pieces, combine):
    while len(jax.tree.leaves(pieces)[0]) > 1:
        pieces = jax.vmap(combine)(*(pieces[side::2] for side in (0, 1)))
    return pieces[0]


def entering(value, axis, combine, identity):
    length, position = (lax.axis_size(axis), lax.axis_index(axis))
    passed = jnp.arange(length) < position

    def kept(part, zero, own):
        part = jnp.where(
            passed.reshape(-1, *(1 for _ in own.shape)), part, jnp.asarray(zero, own.dtype)
        )
        return part

    pieces = from_everyone(value, axis)
    return joined_by_halves(kept(pieces, identity, value), combine)


def taken_together(value, axis):
    return from_everyone(value, axis).sum(axis=0)


def to_tiles(matrix, tile_rows, tile_cols):
    return (
        matrix.reshape(tile_rows, TILE, tile_cols, TILE)
        .transpose(0, 2, 1, 3)
        .reshape(tile_rows * tile_cols, TILE, TILE)
    )


def from_tiles(tiles, tile_rows, tile_cols):
    return (
        tiles.reshape(tile_rows, tile_cols, TILE, TILE)
        .transpose(0, 2, 1, 3)
        .reshape(tile_rows * TILE, tile_cols * TILE)
    )


def mask_tiles(matrix, flags, tile_rows, tile_cols):
    shaped = matrix.reshape(tile_rows, TILE, tile_cols, TILE)
    shaped = shaped * flags[:, None, :, None]
    return shaped.reshape(tile_rows * TILE, tile_cols * TILE)


def compact(tiles, flags_flat, capacity):
    rank_of = jnp.cumsum(flags_flat) - 1
    slot_ids = jnp.arange(capacity, dtype=jnp.int32)
    matched = (flags_flat[None, :] == 1) & (rank_of[None, :] == slot_ids[:, None])
    source = jnp.sum(
        jnp.where(matched, jnp.arange(flags_flat.shape[0], dtype=jnp.int32)[None, :], 0), axis=1
    )
    is_valid = jnp.any(matched, axis=1)
    return jnp.take(tiles, source, axis=0) * is_valid.astype(tiles.dtype)[:, None, None]


def add_up(earlier, later):
    return earlier + later


def shards(a_matrix, a_flags, b_matrix, b_flags, sections):
    tile_rows, panel_cols = a_flags.shape
    tile_cols = b_flags.shape[1]
    row_ratio = lax.axis_size("col") // lax.axis_size("row")
    panel_width = panel_cols * TILE
    a_send_flags = a_flags.astype(jnp.bfloat16)
    product = jnp.zeros((tile_rows * TILE, tile_cols * TILE), jnp.float32)
    intersection = jnp.zeros((tile_rows, tile_cols), jnp.float32)
    for step_index in range(SECTIONS):
        section = sections[step_index]
        owner_row = section // row_ratio
        start_tile = section % row_ratio * panel_cols
        b_panel = lax.dynamic_slice_in_dim(b_matrix, start_tile * TILE, panel_width, 0)
        b_panel_flags = lax.dynamic_slice_in_dim(b_flags, start_tile, panel_cols, 0)
        b_send_flags = b_panel_flags.astype(jnp.bfloat16)
        a_got, a_got_flags = (
            spread(a_matrix, "col", section),
            spread(a_send_flags, "col", section),
        )
        b_got, b_got_flags = (
            broadcast_by_parts(b_panel, "row", owner_row),
            broadcast_by_parts(b_send_flags, "row", owner_row),
        )
        a_masked = mask_tiles(a_got, a_got_flags, tile_rows, panel_cols)
        b_masked = mask_tiles(b_got, b_got_flags, panel_cols, tile_cols)
        product = product + jnp.dot(a_masked, b_masked, preferred_element_type=jnp.float32)
        intersection = intersection + jnp.dot(
            a_got_flags.astype(jnp.float32),
            b_got_flags.astype(jnp.float32),
            precision=lax.Precision.HIGHEST,
        )
    occupied = (intersection > 0.5).astype(jnp.int32).reshape(-1)
    filled = jnp.sum(occupied).reshape(1)
    zero_count = jnp.zeros((1,), jnp.int32)
    within_row = entering(filled, "col", add_up, zero_count)
    row_count = taken_together(filled, "col")
    earlier_rows = entering(row_count, "row", add_up, zero_count)
    offset = within_row + earlier_rows
    tiles = to_tiles(product.astype(jnp.bfloat16), tile_rows, tile_cols)
    packed = from_tiles(compact(tiles, occupied, tile_rows * tile_cols), tile_rows, tile_cols)
    slot_ids = jnp.arange(tile_rows * tile_cols, dtype=jnp.int32)
    places = jnp.where(slot_ids < filled[0], offset[0] + slot_ids, -1).astype(jnp.int32)
    return (packed, places.reshape(tile_rows, tile_cols))


def solution(mesh):
    return jax.shard_map(
        shards,
        mesh=mesh,
        in_specs=(P("row", "col"), P("row", "col"), P("row", "col"), P("row", "col"), P()),
        out_specs=(P("row", "col"), P("row", "col")),
        check_vma=False,
    )
```

profile of v0, /device:TPU:1, one launch (start us, length us, event | category | flops | bytes accessed | tf_op | source)
XLA Modules:
  0.0 321.9 jit_solution(16220235761413224154)
XLA Ops:
  8.0 1.3 fusion.18
  14.8 9.9 %dynamic-slice_select_fusion = (bf16[1024,2048]{1,0:T(8,128)(2,1)}, bf16[1024,2048]{1,0:T(8,128)(2,1)}) fusion(bf16[2048,2048]{1,0:T(8,128)(2,1)} %param.7, s32[]{:T(128)S(6)} %select_n.165, pred[]{:T(512)S(6)} %eq.49, s32[]{:T(128)S(6)} %select_n.160, pred[]{:T(512)S(6)} %eq.47), kind=kLoop, calls=%fused_computation.14 | loop fusion | flops 4194304 | bytes 16777226 | tf_op jit(solution)/shard_map/jit(_where)/select_n | solution.py:23
  24.8 0.7 reduce-scatter.5.cloned.1.call-update
  26.9 6.0 %broadcast_select_fusion = (bf16[2048,1024]{1,0:T(8,128)(2,1)}, bf16[2048,1024]{1,0:T(8,128)(2,1)}) fusion(bf16[2048,1024]{1,0:T(8,128)(2,1)} %param.5, pred[]{:T(512)S(6)} %eq.48, pred[]{:T(512)S(6)} %eq.46), kind=kLoop, calls=%fused_computation.16 | loop fusion | flops 4194304 | bytes 12582914 | tf_op jit(solution)/shard_map/jit(_where)/select_n | solution.py:11
  32.9 30.9 %reduce-scatter.3.cloned.1.call-done = bf16[128,2048]{1,0:T(8,128)(2,1)} async-done(((bf16[1024,2048]{1,0:T(8,128)(2,1)}), bf16[128,2048]{1,0:T(8,128)(2,1)}) %reduce-scatter.3.cloned.1.call-update) | async-done | bytes 524304 | tf_op jit(solution)/shard_map/reduce_scatter | solution.py:27
  63.9 40.2 %reduce-scatter.5.cloned.1.call-done = bf16[128,2048]{1,0:T(8,128)(2,1)} async-done(((bf16[1024,2048]{1,0:T(8,128)(2,1)}), bf16[128,2048]{1,0:T(8,128)(2,1)}) %reduce-scatter.5.cloned.1.call-update) | async-done | bytes 524304 | tf_op jit(solution)/shard_map/reduce_scatter | solution.py:27
  104.2 0.6 dynamic-slice
  104.8 15.4 %all-reduce.4 = (bf16[8,16]{1,0:T(8,128)(2,1)S(1)}, bf16[8,16]{1,0:T(8,128)(2,1)S(1)}) all-reduce(bf16[8,16]{1,0:T(8,128)(2,1)S(1)} %get-tuple-element.15, bf16[8,16]{1,0:T(8,128)(2,1)S(1)} %get-tuple-element.14), channel_id=2, replica_groups=mesh['row'=8,'col'=16] {'row'}, use_global_device_ids=true, to_apply=%region_1.2.clone | all-reduce | flops 256 | bytes 1024
  120.2 0.7 fusion.13
  120.8 9.3 %all-gather = bf16[8,1,16]{2,1,0:T(2,128)(2,1)S(1)} all-gather(bf16[1,1,16]{2,1,0:T(2,128)(2,1)S(1)} %fusion.13), channel_id=1, replica_groups=mesh['row'=8,'col'=16] {'row'}, dimensions={0}, use_global_device_ids=true | all-gather | bytes 288 | tf_op jit(solution)/shard_map/all_gather | solution.py:28
  130.1 0.7 fusion.14
  130.8 10.0 %all-gather.1 = bf16[8,1,16]{2,1,0:T(2,128)(2,1)S(1)} all-gather(bf16[1,1,16]{2,1,0:T(2,128)(2,1)S(1)} %fusion.14), channel_id=1, replica_groups=mesh['row'=8,'col'=16] {'row'}, dimensions={0}, use_global_device_ids=true | all-gather | bytes 288 | tf_op jit(solution)/shard_map/all_gather | solution.py:28
  140.8 34.9 %all-reduce.2 = (bf16[16,8]{0,1:T(8,128)(2,1)S(1)}, bf16[16,8]{0,1:T(8,128)(2,1)S(1)}) all-reduce(bf16[16,8]{0,1:T(8,128)(2,1)S(1)} %get-tuple-element.17, bf16[16,8]{0,1:T(8,128)(2,1)S(1)} %get-tuple-element.16), channel_id=1, replica_groups=mesh['row'=8,'col'=16] {'col'}, use_global_device_ids=true, to_apply=%region_0.1 | all-reduce | flops 256 | bytes 1024 | tf_op jit(solution)/shard_map/psum | solution.py:12
  175.6 0.2 fusion.19
  175.8 0.2 broadcast_compare_fusion
  176.0 0.6 reduce_sum.34
  176.7 1.2 broadcast_in_dim.65
  177.9 3.5 %all-to-all-start = ((s32[16,1,1]{2,1,0:T(1,128)}), s32[16,1,1]{2,1,0:T(1,128)S(1)}, u32[]{:S(2)}, u32[]{:S(2)}) async-start(s32[16,1,1]{2,1,0:T(1,128)} %broadcast_in_dim.65), calls=%async_computation.2 | async-start | bytes 16384 | tf_op jit(solution)/shard_map/all_to_all | solution.py:33
  181.6 0.3 reduce-window.9
  182.1 0.1 slice_reduce_fusion
  182.3 0.1 select_reduce_fusion
  182.6 0.1 fusion.9
  182.8 4.9 %all-to-all-done = s32[16,1,1]{2,1,0:T(1,128)S(1)} async-done(((s32[16,1,1]{2,1,0:T(1,128)}), s32[16,1,1]{2,1,0:T(1,128)S(1)}, u32[]{:S(2)}, u32[]{:S(2)}) %all-to-all-start) | async-done | bytes 96 | tf_op jit(solution)/shard_map/all_to_all | solution.py:33
  187.7 0.9 fusion.15
  188.6 0.1 slice.63
  188.8 0.1 slice.65
  189.0 0.1 slice.67
  189.2 1.2 broadcast_in_dim.67
  190.4 11.3 %all-to-all-start.1 = ((s32[8,1,1]{2,1,0:T(1,128)}), s32[8,1,1]{2,1,0:T(1,128)S(1)}, u32[]{:S(2)}, u32[]{:S(2)}) async-start(s32[8,1,1]{2,1,0:T(1,128)} %broadcast_in_dim.67), calls=%async_computation.3 | async-start | bytes 8192 | tf_op jit(solution)/shard_map/all_to_all | solution.py:33
  201.8 0.6 fusion.17
  203.6 2.6 all-to-all-done.1
  206.3 0.2 reduce.5
  206.7 0.1 slice.73
  206.9 0.6 fusion.16
  208.8 1.3 add_select_fusion
  210.0 0.6 mul.71
  210.6 0.6 mul.67
  211.2 1.0 copy-done.2
  212.2 14.4 %fusion.3 = f32[2048,2048]{1,0:T(8,128)} fusion(bf16[1024,2048]{1,0:T(8,128)(2,1)} %all-gather.5.cloned.1.call-done, bf16[128,8,16,128]{3,2,1,0:T(8,128)(2,1)S(1)} %bitcast.69, bf16[2048,1024]{1,0:T(8,128)(2,1)S(1)} %copy-done.2, bf16[256,8,8,128]{3,2,1,0:T(8,128)(2,1)S(1)} %bitcast.67), kind=kOutput, calls=%fused_computation.10 | convolution fusion | flops 8594128896 | bytes 33554432 | tf_op jit(solution)/shard_map/dot_general | solution.py:122
  226.6 2.6 mul.78
  229.1 2.6 mul.74
  231.7 19.2 %fusion = bf16[256,8,16,128]{3,1,2,0:T(8,128)(2,1)} fusion(f32[2048,2048]{1,0:T(8,128)} %fusion.3, bf16[1024,2048]{1,0:T(8,128)(2,1)} %all-gather.7.cloned.1.call-done, bf16[128,8,16,128]{3,2,1,0:T(8,128)(2,1)} %bitcast.68, bf16[2048,1024]{1,0:T(8,128)(2,1)} %get-tuple-element.7, bf16[256,8,8,128]{3,2,1,0:T(8,128)(2,1)} %bitcast.66), kind=kOutput, calls=%fused_computation.2 | convolution fusion | flops 8602517504 | bytes 41943040 | tf_op jit(solution)/shard_map/dot_general | solution.py:122
  251.0 9.8 %copy.34 = bf16[256,8,16,128]{3,2,1,0:T(8,128)(2,1)} copy(bf16[256,8,16,128]{3,1,2,0:T(8,128)(2,1)} %fusion) | data formatting | bytes 16777216
  260.7 9.3 %copy.26 = bf16[16,128,16,128]{3,1,2,0:T(8,128)(2,1)} copy(bf16[16,128,16,128]{3,2,1,0:T(8,128)(2,1)} %bitcast.63) | data formatting | bytes 16777216 | tf_op jit(solution)/shard_map/reshape | solution.py:62
  270.0 12.0 %gather_fusion = bf16[256,128,128]{2,1,0:T(8,128)(2,1)} fusion(bf16[256,128,128]{2,1,0:T(8,128)(2,1)} %bitcast.62, s32[1024]{0:T(1024)S(1)} %pad_clamp_fusion), kind=kCustom, calls=%fused_computation | custom fusion | bytes 16778240 | tf_op jit(solution)/shard_map/jit(_take)/gather | solution.py:90
  282.0 7.6 %multiply_bitcast_fusion = bf16[16,128,16,128]{3,1,2,0:T(8,128)(2,1)} fusion(bf16[16,16,128,128]{3,2,1,0:T(8,128)(2,1)} %bitcast.61, pred[16,16]{1,0:T(8,128)(4,1)S(1)} %compare_and_fusion, bf16[16,16]{1,0:T(8,128)(2,1)S(1)} %reshape.156), kind=kLoop, calls=%fused_computation.4 | loop fusion | flops 8388608 | bytes 16777984 | tf_op jit(solution)/shard_map/transpose | solution.py:71
  289.6 13.7 %copy.27 = bf16[16,128,16,128]{3,2,1,0:T(8,128)(2,1)} copy(bf16[16,128,16,128]{3,1,2,0:T(8,128)(2,1)} %multiply_bitcast_fusion) | data formatting | bytes 16777216 | tf_op jit(solution)/shard_map/transpose | solution.py:71
  303.3 11.1 %copy.55 = bf16[256,8,16,128]{3,1,2,0:T(8,128)(2,1)} copy(bf16[256,8,16,128]{3,2,1,0:T(8,128)(2,1)} %bitcast.64) | data formatting | bytes 16777216
  (49 shorter events, 1.6 us)
Async XLA Ops:
  8.0 55.9 %reduce-scatter.3.cloned.1.call-start = ((), (), s32[]{:S(2)}) async-start(), calls=%async_computation.4 | async-start | bytes 4718592 | tf_op jit(solution)/shard_map/reduce_scatter | solution.py:27
  24.7 79.4 %reduce-scatter.5.cloned.1.call-start = ((), (), s32[]{:S(2)}) async-start(), calls=%async_computation.6 | async-start | bytes 4718592 | tf_op jit(solution)/shard_map/reduce_scatter | solution.py:27
  25.5 184.6 %all-reduce.7.cloned.1.call-start = ((), (), s32[]{:S(2)}) async-start(), calls=%async_computation.8 | async-start | bytes 16777216 | tf_op jit(solution)/shard_map/psum | solution.py:12
  32.9 71.3 %copy-start.3 = (u32[128]{0:T(128)S(1)}, u32[128]{0:T(128)}, u32[]{:S(2)}) copy-start(u32[128]{0:T(128)} %constant.93) | copy-start | bytes 1540
  32.9 71.9 %copy-start = (s32[16,16]{1,0:T(8,128)S(1)}, s32[16,16]{1,0:T(8,128)}, u32[]{:S(2)}) copy-start(s32[16,16]{1,0:T(8,128)} %param.8) | copy-start | bytes 3076
  32.9 107.9 %copy-start.1 = (s32[16,8]{0,1:T(8,128)S(1)}, s32[16,8]{0,1:T(8,128)}, u32[]{:S(2)}) copy-start(s32[16,8]{0,1:T(8,128)} %param.6) | copy-start | bytes 1540
  32.9 177.1 %all-gather.5.cloned.1.call-start = ((), (), s32[]{:S(2)}) async-start(), calls=%async_computation.5 | async-start | bytes 4718592 | tf_op jit(solution)/shard_map/all_gather | solution.py:28
  63.9 162.7 %all-gather.7.cloned.1.call-start = ((), (), s32[]{:S(2)}) async-start(), calls=%async_computation.7 | async-start | bytes 4718592 | tf_op jit(solution)/shard_map/all_gather | solution.py:28
  177.9 9.8 %all-to-all-start = ((s32[16,1,1]{2,1,0:T(1,128)}), s32[16,1,1]{2,1,0:T(1,128)S(1)}, u32[]{:S(2)}, u32[]{:S(2)}) async-start(s32[16,1,1]{2,1,0:T(1,128)} %broadcast_in_dim.65), calls=%async_computation.2 | async-start | bytes 16384 | tf_op jit(solution)/shard_map/all_to_all | solution.py:33
  190.4 15.8 %all-to-all-start.1 = ((s32[8,1,1]{2,1,0:T(1,128)}), s32[8,1,1]{2,1,0:T(1,128)S(1)}, u32[]{:S(2)}, u32[]{:S(2)}) async-start(s32[8,1,1]{2,1,0:T(1,128)} %broadcast_in_dim.67), calls=%async_computation.3 | async-start | bytes 8192 | tf_op jit(solution)/shard_map/all_to_all | solution.py:33
  210.0 2.2 copy-start.2
Sparse Core Ops, SparseCore 0:
  24.8 39.0 reduce-scatter.2
  66.8 37.2 reduce-scatter.4
  105.9 34.2 all-gather.4
  141.7 32.0 all-gather.6
Sparse Core Ops, SparseCore 1:
  33.0 143.9 all-reduce.6
where the time goes:
time: 327 us; the launch traced here: 322 us
  waiting for transfers between devices  79.3 us (24%)
  local copies, waits for them, and re-layouts  71.6 us (22%)
  blocking collectives  69.5 us (21%)
  matrix products  34 us (10%)
  other arithmetic  27.3 us (8%)
  between operations  25.1 us (8%)
  starting transfers between devices  15 us (5%)
    reduce_scatter x2, waiting for transfers between devices, broadcast_by_parts(): own = lax.psum_scatter(padded, axis, scatter_dimension=0, tiled=True)  71.1 us
    psum x1, blocking collectives, spread(): return lax.psum(kept, axis)  34.9 us
    dot_general x2, matrix products, shards(): jnp.dot(a_masked, b_masked, preferred_element_type=jnp.float32)  33.6 us
    unnamed x15, local copies, waits for them, and re-layouts  23.7 us
    all_gather x2, blocking collectives, broadcast_by_parts(): lax.all_gather(own, axis, axis=0, tiled=True)[:len(lines)]  19.3 us
    unnamed x1, blocking collectives  15.4 us
    all_to_all x2, starting transfers between devices, from_everyone(): return lax.all_to_all(copies, axis, split_axis=0, concat_axis=0, tiled=True)  14.8 us
    transpose x1, local copies, waits for them, and re-layouts, from_tiles(): return tiles.reshape(tile_rows, tile_cols, TILE, TILE).transpose(0, 2, 1,...  13.7 us
  transfers between devices with their start and end apart: 7, of which 4 were waited for; matrix products, arithmetic and copies ran while one was open for 10% of the time, Pallas kernels for 0%

commit v1 on v0

v1 whole, which is shorter than its diff:
```python
import jax
import jax.numpy as jnp
from jax import lax
from jax.experimental import pallas as pl
from jax.experimental.pallas import tpu as pltpu
from jax.sharding import PartitionSpec as P

TILE = 128
KT = 8
MOST = 64
N_ROW = 8
N_COL = 16
B_LANE = 16
MESH = pl.DeviceIdType.MESH
VMEM = pl.BlockSpec(memory_space=pltpu.VMEM)
SMEM = pl.BlockSpec(memory_space=pltpu.SMEM)
ANY = pl.BlockSpec(memory_space=pl.ANY)


def tiles_of(*lead):
    return (*lead, TILE, TILE)


def pack_kernel(sec, af, bf, af_v, bf_v, a_hbm, b_hbm, pa, pb, msg, src_a, src_b0, src_b1, sems):
    def listed(flag_at, count, src):
        def step(i, found):
            src[found] = i
            return found + flag_at(i)

        return lax.fori_loop(0, count, step, jnp.int32(0), unroll=8)

    def copy_of(matrix, row, col, dst, sem):
        return pltpu.make_async_copy(
            matrix.at[pl.ds(pl.multiple_of(row * TILE, TILE), TILE), pl.ds(pl.multiple_of(col * TILE, TILE), TILE)],
            dst,
            sem,
        )

    def start_a():
        found = listed(lambda i: af[i // KT, i % KT], 16 * KT, src_a)

        def go(j, _):
            i = jnp.where(j < found, src_a[j], 0)
            copy_of(a_hbm, i // KT, i % KT, pa.at[j], sems.at[0]).start()
            return 0

        lax.fori_loop(0, MOST, go, 0, unroll=4)

    def start_b(s, src):
        first = (sec[s] % 2) * KT
        found = listed(lambda i: bf[first + i // 16, i % 16], 16 * KT, src)

        def go(j, _):
            i = jnp.where(j < found, src[j], 0)
            copy_of(b_hbm, first + i // 16, i % 16, pb.at[s, j], sems.at[1 + s]).start()
            return 0

        lax.fori_loop(0, MOST, go, 0, unroll=4)

    start_b(0, src_b0)
    start_b(1, src_b1)
    start_a()
    msg[...] = jnp.zeros_like(msg)
    msg[:, 0:KT] = af_v[...]
    msg[:, B_LANE : B_LANE + 16] = bf_v[...]
    pltpu.make_async_copy(pb.at[0], pb.at[0], sems.at[1]).wait()
    pltpu.make_async_copy(pb.at[1], pb.at[1], sems.at[2]).wait()
    pltpu.make_async_copy(pa, pa, sems.at[0]).wait()


def packed_panels(sections, a_flags, b_flags, a_matrix, b_matrix):
    return pl.pallas_call(
        pack_kernel,
        out_shape=(
            jax.ShapeDtypeStruct(tiles_of(MOST), jnp.bfloat16),
            jax.ShapeDtypeStruct(tiles_of(2, MOST), jnp.bfloat16),
            jax.ShapeDtypeStruct((16, 128), jnp.int32),
        ),
        in_specs=[SMEM, SMEM, SMEM, VMEM, VMEM, ANY, ANY],
        out_specs=(VMEM, VMEM, VMEM),
        scratch_shapes=[
            pltpu.SMEM((136,), jnp.int32),
            pltpu.SMEM((136,), jnp.int32),
            pltpu.SMEM((136,), jnp.int32),
            pltpu.SemaphoreType.DMA((3,)),
        ],
        compiler_params=pltpu.CompilerParams(vmem_limit_bytes=24 << 20),
        name="pack",
    )(sections, a_flags, b_flags, a_flags, b_flags, a_matrix, b_matrix)


N_SEMS = 160


def exchange_kernel(
    sec, pa, pb, msg,
    af, bf, afl, bfl, off,
    cand_0, cand_1, trans, pick, cand2_0, cand2_1, trans2,
    x_buf, y_buf, z_tr, z_dir, z_mg, z_send,
    f_a, f_b, c_a, c_b, cnt, tot,
    send_sems, recv_sems,
):
    cand, cand2 = (cand_0, cand_1), (cand2_0, cand2_1)
    r, c = lax.axis_index("row"), lax.axis_index("col")
    z, core = r // 2, r % 2
    y, x = c // 4, c % 4
    pos = {"x": x, "y": y, "z": z}

    def at(dim, step):
        where = dict(pos)
        where[dim] = (pos[dim] + step) % 4
        return (where["z"] * 2 + core, where["y"] * 4 + where["x"])

    partner = (z * 2 + 1 - core, c)
    col_peers = [(r, (c + d) % N_COL) for d in range(1, N_COL)]
    row_peers = [((r + d) % N_ROW, c) for d in range(1, N_ROW)]

    barrier = pltpu.get_barrier_semaphore()
    for peer in col_peers + row_peers:
        pl.semaphore_signal(barrier, inc=1, device_id=peer, device_id_type=MESH)
    pl.semaphore_wait(barrier, len(col_peers) + len(row_peers))

    started = []

    def send(src, dst, peer):
        n = len(started)
        copy = pltpu.make_async_remote_copy(
            src_ref=src, dst_ref=dst, send_sem=send_sems.at[n], recv_sem=recv_sems.at[n],
            device_id=peer, device_id_type=MESH,
        )
        copy.start()
        started.append(copy)
        return copy

    sec_v = [sec[0], sec[1]]
    root = [{"x": lax.rem(v, 4), "y": lax.div(v, 4), "z": lax.div(v, 4)} for v in sec_v]
    root_core = [lax.rem(lax.div(v, 2), 2) for v in sec_v]

    flags_row = [send(msg, f_a.at[c], peer) for peer in col_peers]
    flags_col = [send(msg, f_b.at[r], peer) for peer in row_peers]

    axes = (("x", "y"), ("y", "x"))
    a1 = []
    for h in range(2):
        d, p = axes[h][0], pos[axes[h][0]]
        far = h * 32 + ((p + 2) % 4) * 8
        a1.append([
            send(pa.at[pl.ds(far, 4)], trans.at[h, 0], at(d, 1)),
            send(pa.at[pl.ds(far + 4, 4)], trans.at[h, 1], at(d, 3)),
        ])
    b0 = [send(pb.at[s, pl.ds((1 - core) * 32, 32)], x_buf.at[s, core], partner) for s in range(2)]
    for h in range(2):
        d, p = axes[h][0], pos[axes[h][0]]
        a1[h] += [
            send(pa.at[pl.ds(h * 32 + ((p + 1) % 4) * 8, 8)], cand[h].at[p], at(d, 1)),
            send(pa.at[pl.ds(h * 32 + ((p + 3) % 4) * 8, 8)], cand[h].at[p], at(d, 3)),
        ]
    f_a[c] = msg[...]
    f_b[r] = msg[...]
    for s in range(2):
        x_buf[s, core] = pb[s, pl.ds(core * 32, 32)]
    for h in range(2):
        p = pos[axes[h][0]]
        cand[h][p] = pa[pl.ds(h * 32 + p * 8, 8)]

    for copy in flags_row + flags_col:
        copy.wait_recv()
    inter = jnp.zeros((16, 128), jnp.int32)
    for s in range(2):
        a_own = f_a[sec_v[s]]
        b_pair = f_b[lax.div(sec_v[s], 2)]
        b_own = jnp.where(lax.rem(sec_v[s], 2) == 0, b_pair[0:KT], b_pair[KT:])
        afl[s] = a_own
        bfl[s] = b_own
        for k in range(KT):
            inter = inter + a_own[:, k : k + 1] * b_own[k : k + 1, :]
    lane = lax.broadcasted_iota(jnp.int32, (16, 128), 1)
    held = (inter > 0) & (lane >= B_LANE) & (lane < B_LANE + 16)
    filled = jnp.sum(jnp.where(held, 1, 0), axis=(0, 1), keepdims=True)
    cnt[...] = jnp.broadcast_to(filled, (8, 128))
    counts = [send(cnt, c_a.at[c], peer) for peer in col_peers]
    c_a[c] = cnt[...]

    for copy in b0:
        copy.wait_recv()
    for s in range(2):
        for i in range(8):
            y_buf[i, s] = x_buf[s, root_core[s], i * 4 : i * 4 + 4]
    w = z
    b1 = [
        send(y_buf.at[((w + 2) % 4) * 2], z_tr.at[0], at("z", 1)),
        send(y_buf.at[((w + 2) % 4) * 2 + 1], z_tr.at[1], at("z", 3)),
        send(y_buf.at[((w + 1) % 4) * 2 + 1], z_dir.at[1], at("z", 1)),
        send(y_buf.at[((w + 3) % 4) * 2], z_dir.at[0], at("z", 3)),
    ]

    for h in range(2):
        d, p = axes[h][0], pos[axes[h][0]]
        a1[h][0].wait_recv()
        a1[h].append(send(trans.at[h, 0], cand[h].at[(p + 3) % 4, pl.ds(0, 4)], at(d, 1)))
        a1[h][1].wait_recv()
        a1[h].append(send(trans.at[h, 1], cand[h].at[(p + 1) % 4, pl.ds(4, 4)], at(d, 3)))

    for copy in counts:
        copy.wait_recv()
    place = lax.broadcasted_iota(jnp.int32, (N_COL, 8, 128), 0)
    all_counts = c_a[...]
    within = jnp.sum(jnp.where(place < c, all_counts, 0), axis=0)
    tot[...] = jnp.sum(all_counts, axis=0)
    totals = [send(tot, c_b.at[r], peer) for peer in row_peers]
    c_b[r] = tot[...]

    a2 = []
    for h in range(2):
        for n in (2, 3, 4, 5):
            a1[h][n].wait_recv()
        d, q = axes[h][1], pos[axes[h][1]]
        for s in range(2):
            for j in range(8):
                pick[h, j, s] = cand[h][root[s][axes[h][0]], j]
        far = ((q + 2) % 4) * 2
        a2.append([
            send(pick.at[h, far], trans2.at[h, 0], at(d, 1)),
            send(pick.at[h, far + 1], trans2.at[h, 1], at(d, 3)),
            send(pick.at[h, pl.ds(((q + 1) % 4) * 2, 2)], cand2[h].at[q], at(d, 1)),
            send(pick.at[h, pl.ds(((q + 3) % 4) * 2, 2)], cand2[h].at[q], at(d, 3)),
        ])
        cand2[h][q] = pick[h, pl.ds(q * 2, 2)]

    def z_merged(t, own_at):
        for s in range(2):
            here = root[s]["z"] == w
            z_send[t, s] = jnp.where(here, y_buf[own_at, s], z_tr[t, s])

    b1[0].wait_recv()
    z_merged(0, ((w + 1) % 4) * 2)
    b1.append(send(z_send.at[0], z_mg.at[0], at("z", 1)))
    b1[1].wait_recv()
    z_merged(1, ((w + 3) % 4) * 2 + 1)
    b1.append(send(z_send.at[1], z_mg.at[1], at("z", 3)))

    for h in range(2):
        d, q = axes[h][1], pos[axes[h][1]]
        a2[h][0].wait_recv()
        a2[h].append(send(trans2.at[h, 0], cand2[h].at[(q + 3) % 4, 0], at(d, 1)))
        a2[h][1].wait_recv()
        a2[h].append(send(trans2.at[h, 1], cand2[h].at[(q + 1) % 4, 1], at(d, 3)))

    def a_slot(h, p, q):
        return h * 32 + p * 8 + q * 2

    a3 = []
    for h in range(2):
        for n in (2, 3, 4, 5):
            a2[h][n].wait_recv()
        p, (d, q) = pos[axes[h][0]], (axes[h][1], pos[axes[h][1]])
        own = a_slot(h, p, q)
        for s in range(2):
            for t in range(2):
                af[own + t, s] = cand2[h][root[s][d], t, s]
        block = af.at[pl.ds(own, 2)]
        a3.append([send(block, block, at(d, 1)), send(block, block, at(d, 3))])

    a4 = []

    def a_out(h, e):
        d, p = axes[h][0], pos[axes[h][0]]
        q = (pos[axes[h][1]] - e) % 4
        block = af.at[pl.ds(a_slot(h, p, q), 2)]
        a4.append((h, q, send(block, block, at(d, 1)), send(block, block, at(d, 3))))

    for h in range(2):
        a_out(h, 0)
    for h in range(2):
        d, p, q = axes[h][1], pos[axes[h][0]], pos[axes[h][1]]
        a3[h][0].wait_recv()
        part = af.at[a_slot(h, p, (q + 3) % 4)]
        a3[h].append(send(part, part, at(d, 1)))
        a3[h][1].wait_recv()
        part = af.at[a_slot(h, p, (q + 1) % 4) + 1]
        a3[h].append(send(part, part, at(d, 3)))
    for e in (1, 3):
        for h in range(2):
            a_out(h, e)

    b1[4].wait_recv()
    b1[5].wait_recv()
    b1[2].wait_recv()
    b1[3].wait_recv()
    mine = core * 8 + w * 2
    for t in range(2):
        for s in range(2):
            ahead = lax.rem(root[s]["z"] - w + 4, 4)
            near = 1 if t == 0 else 3
            got = jnp.where(ahead == near, z_dir[t, s], z_mg[t, s])
            bf[mine + t, s] = jnp.where(ahead == 0, y_buf[w * 2 + t, s], got)

    b2 = {}
    b3 = []

    def b_part(step, t):
        return bf.at[core * 8 + ((w + step) % 4) * 2 + t]

    for t in range(2):
        ref = b_part(0, t)
        b2["up", t] = send(ref, ref, at("z", 1))
        ref = b_part(0, 1 - t)
        b2["down", 1 - t] = send(ref, ref, at("z", 3))
    for t in range(2):
        ref = b_part(0, t)
        b3.append(send(ref, ref, partner))

    for h in range(2):
        a3[h][2].wait_recv()
        a3[h][3].wait_recv()
        a_out(h, 2)

    a5 = []

    def a_forward(n):
        h, q, up, down = a4[n]
        d, p = axes[h][0], pos[axes[h][0]]
        up.wait_recv()
        part = af.at[a_slot(h, (p + 3) % 4, q)]
        a5.append(send(part, part, at(d, 1)))
        down.wait_recv()
        part = af.at[a_slot(h, (p + 1) % 4, q) + 1]
        a5.append(send(part, part, at(d, 3)))

    for n in range(4):
        a_forward(n)
    b2["up", 0].wait_recv()
    ref = b_part(3, 0)
    b2["up", 2] = send(ref, ref, at("z", 1))
    b3.append(send(ref, ref, partner))
    b2["down", 1].wait_recv()
    ref = b_part(1, 1)
    b2["down", 2] = send(ref, ref, at("z", 3))
    b3.append(send(ref, ref, partner))
    for n in range(4, 8):
        a_forward(n)
    for key, step, t in ((("up", 1), 3, 1), (("down", 0), 1, 0), (("up", 2), 2, 0), (("down", 2), 2, 1)):
        b2[key].wait_recv()
        ref = b_part(step, t)
        b3.append(send(ref, ref, partner))

    for copy in totals:
        copy.wait_recv()
    place = lax.broadcasted_iota(jnp.int32, (N_ROW, 8, 128), 0)
    off[...] = within + jnp.sum(jnp.where(place < r, c_b[...], 0), axis=0)

    for copy in a5 + b3:
        copy.wait_recv()
    for copy in started:
        copy.wait_send()


def exchanged(sections, pa, pb, msg):
    bf16, i32 = jnp.bfloat16, jnp.int32
    return pl.pallas_call(
        exchange_kernel,
        out_shape=(
            jax.ShapeDtypeStruct(tiles_of(MOST, 2), bf16),
            jax.ShapeDtypeStruct(tiles_of(16, 2, 4), bf16),
            jax.ShapeDtypeStruct((2, 16, 128), i32),
            jax.ShapeDtypeStruct((2, KT, 128), i32),
            jax.ShapeDtypeStruct((8, 128), i32),
        ),
        in_specs=[SMEM, VMEM, VMEM, VMEM],
        out_specs=(VMEM,) * 5,
        scratch_shapes=[
            pltpu.VMEM(tiles_of(4, 8), bf16),
            pltpu.VMEM(tiles_of(4, 8), bf16),
            pltpu.VMEM(tiles_of(2, 2, 4), bf16),
            pltpu.VMEM(tiles_of(2, 8, 2), bf16),
            pltpu.VMEM(tiles_of(4, 2, 2), bf16),
            pltpu.VMEM(tiles_of(4, 2, 2), bf16),
            pltpu.VMEM(tiles_of(2, 2, 2), bf16),
            pltpu.VMEM(tiles_of(2, 2, 32), bf16),
            pltpu.VMEM(tiles_of(8, 2, 4), bf16),
            pltpu.VMEM(tiles_of(2, 2, 4), bf16),
            pltpu.VMEM(tiles_of(2, 2, 4), bf16),
            pltpu.VMEM(tiles_of(2, 2, 4), bf16),
            pltpu.VMEM(tiles_of(2, 2, 4), bf16),
            pltpu.VMEM((N_COL, 16, 128), i32),
            pltpu.VMEM((N_ROW, 16, 128), i32),
            pltpu.VMEM((N_COL, 8, 128), i32),
            pltpu.VMEM((N_ROW, 8, 128), i32),
            pltpu.VMEM((8, 128), i32),
            pltpu.VMEM((8, 128), i32),
            pltpu.SemaphoreType.DMA((N_SEMS,)),
            pltpu.SemaphoreType.DMA((N_SEMS,)),
        ],
        compiler_params=pltpu.CompilerParams(collective_id=0, has_side_effects=True, vmem_limit_bytes=48 << 20),
        name="exchange",
    )(sections, pa, pb, msg)


def product_kernel(af, bf, afl, bfl, off, packed, places, b_dense, a_rows, staged, masks, sems):
    def unpack_b(n, counts):
        s, k = n // KT, n % KT
        count = jnp.where(k == 0, 0, counts)
        mask = jnp.int32(0)
        for q in range(16):
            flag = bfl[s, k, B_LANE + q]
            tile = bf[count // 4, s, count % 4]
            b_dense[pl.ds(pl.multiple_of(n * TILE, TILE), TILE), q * TILE : (q + 1) * TILE] = jnp.where(
                flag > 0, tile, jnp.zeros_like(tile)
            )
            count = jnp.minimum(count + flag, MOST - 1)
            mask = mask + flag * (1 << q)
        masks[n] = mask
        return count

    lax.fori_loop(0, 2 * KT, unpack_b, jnp.int32(0))

    def row_copy(i):
        rows = pl.ds(pl.multiple_of(i * TILE, TILE), TILE)
        return pltpu.make_async_copy(staged.at[rows], packed.at[rows], sems.at[i])

    def store(slot, tile):
        rows = pl.ds(pl.multiple_of(slot // 16 * TILE, TILE), TILE)
        cols = pl.ds(pl.multiple_of(slot % 16 * TILE, TILE), TILE)
        staged[rows, cols] = tile

    def two_rows(p2, carry):
        count0, count1, slot, done = carry
        counts = [count0, count1]
        row_masks = []
        for pp in range(2):
            mask = jnp.int32(0)
            for s in range(2):
                for k in range(KT):
                    flag = afl[s, p2 * 2 + pp, k]
                    tile = af[counts[s], s]
                    n = s * KT + k
                    a_rows[pp * TILE : (pp + 1) * TILE, n * TILE : (n + 1) * TILE] = jnp.where(
                        flag > 0, tile, jnp.zeros_like(tile)
                    )
                    counts[s] = jnp.minimum(counts[s] + flag, MOST - 1)
                    mask = mask | (masks[n] * flag)
            row_masks.append(mask)
        ahead = jnp.int32(0)
        for q in range(16):
            ahead = ahead + ((row_masks[0] >> q) & 1)
        slots = (slot, slot + ahead)

        def columns(n, slots):
            lhs = a_rows[...]
            rhs = b_dense[:, pl.ds(pl.multiple_of(n * 512, 512), 512)]
            out = jnp.dot(lhs, rhs, preferred_element_type=jnp.float32).astype(jnp.bfloat16)
            slots = list(slots)
            for pp in range(2):
                for q in range(4):
                    bit = (row_masks[pp] >> (n * 4 + q)) & 1

                    @pl.when(bit > 0)
                    def _(pp=pp, q=q, slot=slots[pp]):
                        store(slot, out[pp * TILE : (pp + 1) * TILE, q * TILE : (q + 1) * TILE])

                    slots[pp] = slots[pp] + bit
            return tuple(slots)

        _, slot = lax.fori_loop(0, 4, columns, slots)
        ready = slot // 16

        def out_row(i, _):
            row_copy(i).start()
            return 0

        lax.fori_loop(done, ready, out_row, 0)
        return counts[0], counts[1], slot, ready

    zero = jnp.int32(0)
    _, _, slot, done = lax.fori_loop(0, 8, two_rows, (zero, zero, zero, zero))

    def blank(i, _):
        store(i, jnp.zeros((TILE, TILE), jnp.bfloat16))
        return 0

    lax.fori_loop(slot, 256, blank, 0)

    def out_row(i, _):
        row_copy(i).start()
        return 0

    lax.fori_loop(done, 16, out_row, 0)
    index = lax.broadcasted_iota(jnp.int32, (16, 16), 0) * 16 + lax.broadcasted_iota(jnp.int32, (16, 16), 1)
    places[...] = jnp.where(index < slot, index + off[0:1, 0:1], -1)
    for i in range(16):
        row_copy(i).wait()


def products(af, bf, afl, bfl, off):
    return pl.pallas_call(
        product_kernel,
        out_shape=(
            jax.ShapeDtypeStruct((2048, 2048), jnp.bfloat16),
            jax.ShapeDtypeStruct((16, 16), jnp.int32),
        ),
        in_specs=[VMEM, VMEM, SMEM, SMEM, VMEM],
        out_specs=(ANY, VMEM),
        scratch_shapes=[
            pltpu.VMEM((2048, 2048), jnp.bfloat16),
            pltpu.VMEM((256, 2048), jnp.bfloat16),
            pltpu.VMEM((2048, 2048), jnp.bfloat16),
            pltpu.SMEM((16,), jnp.int32),
            pltpu.SemaphoreType.DMA((16,)),
        ],
        compiler_params=pltpu.CompilerParams(vmem_limit_bytes=48 << 20),
        name="product",
    )(af, bf, afl, bfl, off)


def shards(a_matrix, a_flags, b_matrix, b_flags, sections):
    pa, pb, msg = packed_panels(sections, a_flags, b_flags, a_matrix, b_matrix)
    return products(*exchanged(sections, pa, pb, msg))


def solution(mesh):
    return jax.shard_map(
        shards,
        mesh=mesh,
        in_specs=(P("row", "col"), P("row", "col"), P("row", "col"), P("row", "col"), P()),
        out_specs=(P("row", "col"), P("row", "col")),
        check_vma=False,
    )
```

time: 327 us -> 125 us (0.38); the launches traced: 322 us -> 125 us
  Pallas kernels: 0 us -> 113 us
  waiting for transfers between devices: 79.3 us -> 0 us
  blocking collectives: 69.5 us -> 0 us
  local copies, waits for them, and re-layouts: 71.6 us -> 11.9 us
  matrix products: 34 us -> 0 us
  other arithmetic: 27.3 us -> 0 us
  between operations: 25.1 us -> 0.67 us
  starting transfers between devices: 15 us -> 0 us
    pallas_call x0 -> x3, Pallas kernels: none -> 113 us  [the longest x1 64.8 us: exchanged(): pl.pallas_call(exchange_kernel, out_shape=(jax.ShapeDtypeStruct(tiles_of(...]
    reduce_scatter x2 -> x0, waiting for transfers between devices: 71.1 us -> none  [broadcast_by_parts(): own = lax.psum_scatter(padded, axis, scatter_dimension=0, tiled=True)]
    psum x1 -> x0, blocking collectives: 34.9 us -> none  [spread(): return lax.psum(kept, axis)]
    dot_general x4 -> x0, matrix products: 34 us -> none  [the longest x2 33.6 us: shards(): jnp.dot(a_masked, b_masked, preferred_element_type=jnp.float32)]
    all_gather x2 -> x0, blocking collectives: 19.3 us -> none  [broadcast_by_parts(): lax.all_gather(own, axis, axis=0, tiled=True)[:len(lines)]]
    select_n x8 -> x0, other arithmetic: 17.2 us -> none  [the longest x2 9.91 us: broadcast_by_parts(): jnp.where(lax.axis_index(axis) == root, value, jnp.zeros_like(value))]
    unnamed x1 -> x0, blocking collectives: 15.4 us -> none
    all_to_all x2 -> x0, starting transfers between devices: 14.8 us -> none  [from_everyone(): return lax.all_to_all(copies, axis, split_axis=0, concat_axis=0, tiled=True)]
  transfers between devices with their start and end apart: 7 -> 0, of which waited for: 4 -> 0; matrix products, arithmetic and copies ran while one was open for 10% -> 0% of each run, Pallas kernels for 0% -> 0%
where the time goes in v1:
time: 125 us
  Pallas kernels  113 us (90%)
  local copies, waits for them, and re-layouts  11.9 us (10%)
    pallas_call x1, Pallas kernels, exchanged(): pl.pallas_call(exchange_kernel, out_shape=(jax.ShapeDtypeStruct(tiles_of(...  64.8 us
    pallas_call x1, Pallas kernels, products(): pl.pallas_call(product_kernel, out_shape=(jax.ShapeDtypeStruct((2048, 204...  39.5 us
    unnamed x15, local copies, waits for them, and re-layouts  11.9 us
    pallas_call x1, Pallas kernels, packed_panels(): pl.pallas_call(pack_kernel, out_shape=(jax.ShapeDtypeStruct(tiles_of(MOST...  8.66 us

profile of v1, /device:TPU:1, one launch (start us, length us, event | category | flops | bytes accessed | tf_op | source)
XLA Modules:
  0.0 125.5 jit_solution(6842674285886215919)
XLA Ops:
  0.6 0.8 copy.7.af.af_v
  1.4 0.0 copy-start
  1.4 3.4 %copy-done = bf16[2048,2048]{1,0:T(8,128)(2,1)S(1)} copy-done((bf16[2048,2048]{1,0:T(8,128)(2,1)S(1)}, bf16[2048,2048]{1,0:T(8,128)(2,1)}, u32[]{:S(2)}) %copy-start) | copy-done | bytes 8388632
  4.8 0.0 copy-start.2
  4.8 2.2 %copy-done.2 = bf16[2048,1024]{1,0:T(8,128)(2,1)S(1)} copy-done((bf16[2048,1024]{1,0:T(8,128)(2,1)S(1)}, bf16[2048,1024]{1,0:T(8,128)(2,1)}, u32[]{:S(2)}) %copy-start.2) | copy-done | bytes 4194328
  7.0 0.0 copy-start.4
  7.0 0.7 copy-done.4
  7.7 0.0 copy-start.5
  7.7 0.7 copy-done.5
  8.3 0.0 copy-start.6
  8.3 8.7 %pack.1 = (bf16[64,128,128]{2,1,0:T(8,128)(2,1)S(1)}, bf16[2,64,128,128]{3,2,1,0:T(8,128)(2,1)S(1)}, s32[16,128]{1,0:T(8,128)S(1)}) custom-call(s32[2]{0:T(128)S(1)} %copy-done.5, s32[16,8]{1,0:T(8,128)S(1)} %copy.7.af.af_v, s32[16,16]{1,0:T(8,128)S(1)} %copy-done.4, s32[16,8]{1,0:T(8,128)S(1)} %copy.7.af.af_v, s32[16,16]{1,0:T(8,128)S(1)} %copy-done.4, ...), custom_call_target="tpu_custom_call" | custom-call | tf_op jit(solution)/shard_map/pack/pallas_call | solution.py:72
  17.0 0.0 copy-start.1
  17.0 2.0 %copy-done.1 = bf16[2,64,128,128]{3,2,1,0:T(8,128)(2,1)} copy-done((bf16[2,64,128,128]{3,2,1,0:T(8,128)(2,1)}, bf16[2,64,128,128]{3,2,1,0:T(8,128)(2,1)S(1)}, u32[]{:S(2)}) %copy-start.1) | copy-done | bytes 4194328
  19.0 0.0 copy-done.6
  19.0 64.8 %exchange.1 = (bf16[64,2,128,128]{3,2,1,0:T(8,128)(2,1)}, bf16[16,2,4,128,128]{4,3,2,1,0:T(8,128)(2,1)}, s32[2,16,128]{2,1,0:T(8,128)S(1)}, s32[2,8,128]{2,1,0:T(8,128)S(1)}, s32[8,128]{1,0:T(8,128)S(1)}) custom-call(s32[2]{0:T(128)S(1)} %copy-done.6, bf16[64,128,128]{2,1,0:T(8,128)(2,1)S(1)} %get-tuple-element.10.pa, bf16[2,64,128,128]{3,2,1,0:T(8,128)(2,1)} %copy-done.1, ...), custom_call_target="tpu_custom_call" | custom-call | tf_op jit(solution)/shard_map/exchange/pallas_call | solution.py:360
  83.8 0.0 copy-start.3
  83.8 2.2 %copy-done.3 = bf16[64,2,128,128]{3,2,1,0:T(8,128)(2,1)S(1)} copy-done((bf16[64,2,128,128]{3,2,1,0:T(8,128)(2,1)S(1)}, bf16[64,2,128,128]{3,2,1,0:T(8,128)(2,1)}, u32[]{:S(2)}) %copy-start.3) | copy-done | bytes 4194328
  86.0 39.5 %product.1 = (bf16[2048,2048]{1,0:T(8,128)(2,1)}, s32[16,16]{1,0:T(8,128)}) custom-call(bf16[64,2,128,128]{3,2,1,0:T(8,128)(2,1)S(1)} %copy-done.3, bf16[16,2,4,128,128]{4,3,2,1,0:T(8,128)(2,1)} %get-tuple-element.14.bf, s32[2,16,128]{2,1,0:T(8,128)S(1)} %get-tuple-element.15.afl, s32[2,8,128]{2,1,0:T(8,128)S(1)} %get-tuple-element.16.bfl, ...), custom_call_target="tpu_custom_call" | custom-call | tf_op jit(solution)/shard_map/product/pallas_call | solution.py:495
Async XLA Ops:
  1.4 3.4 %copy-start = (bf16[2048,2048]{1,0:T(8,128)(2,1)S(1)}, bf16[2048,2048]{1,0:T(8,128)(2,1)}, u32[]{:S(2)}) copy-start(bf16[2048,2048]{1,0:T(8,128)(2,1)} %b_hbm.1) | copy-start | bytes 25165828
  4.8 2.2 %copy-start.2 = (bf16[2048,1024]{1,0:T(8,128)(2,1)S(1)}, bf16[2048,1024]{1,0:T(8,128)(2,1)}, u32[]{:S(2)}) copy-start(bf16[2048,1024]{1,0:T(8,128)(2,1)} %a_hbm.1) | copy-start | bytes 12582916
  7.0 0.7 copy-start.4
  7.7 0.7 copy-start.5
  8.3 10.7 %copy-start.6 = (s32[2]{0:T(128)S(1)}, s32[2]{0:T(128)}, u32[]{:S(2)}) copy-start(s32[2]{0:T(128)} %sec.3) | copy-start | bytes 28
  17.0 2.0 %copy-start.1 = (bf16[2,64,128,128]{3,2,1,0:T(8,128)(2,1)}, bf16[2,64,128,128]{3,2,1,0:T(8,128)(2,1)S(1)}, u32[]{:S(2)}) copy-start(bf16[2,64,128,128]{3,2,1,0:T(8,128)(2,1)S(1)} %get-tuple-element.11.pb) | copy-start | bytes 12582916
  83.8 2.2 %copy-start.3 = (bf16[64,2,128,128]{3,2,1,0:T(8,128)(2,1)S(1)}, bf16[64,2,128,128]{3,2,1,0:T(8,128)(2,1)}, u32[]{:S(2)}) copy-start(bf16[64,2,128,128]{3,2,1,0:T(8,128)(2,1)} %get-tuple-element.13.af) | copy-start | bytes 12582916

commit v2 on v1

--- a/solution.py
+++ b/solution.py
@@ -14,14 +14,25 @@
 MESH = pl.DeviceIdType.MESH
 VMEM = pl.BlockSpec(memory_space=pltpu.VMEM)
 SMEM = pl.BlockSpec(memory_space=pltpu.SMEM)
-ANY = pl.BlockSpec(memory_space=pl.ANY)
+HBM = pl.BlockSpec(memory_space=pltpu.HBM)
 
 
 def tiles_of(*lead):
     return (*lead, TILE, TILE)
 
 
-def pack_kernel(sec, af, bf, af_v, bf_v, a_hbm, b_hbm, pa, pb, msg, src_a, src_b0, src_b1, sems):
+def pack_kernel(
+    sec_h, af_h, bf_h, a_hbm, b_hbm, pa, pb, msg, sec, af, bf, af_v, bf_v, src_a, src_b0, src_b1, sems, small
+):
+    fetched = [
+        pltpu.make_async_copy(src, dst, small.at[n])
+        for n, (src, dst) in enumerate(
+            ((sec_h, sec), (bf_h, bf), (af_h, af), (af_h, af_v), (bf_h, bf_v))
+        )
+    ]
+    for copy in fetched:
+        copy.start()
+
     def listed(flag_at, count, src):
         def step(i, found):
             src[found] = i
@@ -57,9 +68,13 @@
 
         lax.fori_loop(0, MOST, go, 0, unroll=4)
 
+    for copy in fetched[:3]:
+        copy.wait()
     start_b(0, src_b0)
     start_b(1, src_b1)
     start_a()
+    for copy in fetched[3:]:
+        copy.wait()
     msg[...] = jnp.zeros_like(msg)
     msg[:, 0:KT] = af_v[...]
     msg[:, B_LANE : B_LANE + 16] = bf_v[...]
@@ -72,21 +87,27 @@
     return pl.pallas_call(
         pack_kernel,
         out_shape=(
-            jax.ShapeDtypeStruct(tiles_of(MOST), jnp.bfloat16),
-            jax.ShapeDtypeStruct(tiles_of(2, MOST), jnp.bfloat16),
-            jax.ShapeDtypeStruct((16, 128), jnp.int32),
+            pltpu.VMEM(tiles_of(MOST), jnp.bfloat16),
+            pltpu.VMEM(tiles_of(2, MOST), jnp.bfloat16),
+            pltpu.VMEM((16, 128), jnp.int32),
         ),
-        in_specs=[SMEM, SMEM, SMEM, VMEM, VMEM, ANY, ANY],
+        in_specs=[HBM] * 5,
         out_specs=(VMEM, VMEM, VMEM),
         scratch_shapes=[
+            pltpu.SMEM((2,), jnp.int32),
+            pltpu.SMEM((16, KT), jnp.int32),
+            pltpu.SMEM((16, 16), jnp.int32),
+            pltpu.VMEM((16, KT), jnp.int32),
+            pltpu.VMEM((16, 16), jnp.int32),
             pltpu.SMEM((136,), jnp.int32),
             pltpu.SMEM((136,), jnp.int32),
             pltpu.SMEM((136,), jnp.int32),
             pltpu.SemaphoreType.DMA((3,)),
+            pltpu.SemaphoreType.DMA((6,)),
         ],
-        compiler_params=pltpu.CompilerParams(vmem_limit_bytes=24 << 20),
+        compiler_params=pltpu.CompilerParams(vmem_limit_bytes=16 << 20),
         name="pack",
-    )(sections, a_flags, b_flags, a_flags, b_flags, a_matrix, b_matrix)
+    )(*(pltpu.with_memory_space_constraint(v, pltpu.HBM) for v in (sections, a_flags, b_flags, a_matrix, b_matrix)))
 
 
 N_SEMS = 160
@@ -360,11 +381,11 @@
     return pl.pallas_call(
         exchange_kernel,
         out_shape=(
-            jax.ShapeDtypeStruct(tiles_of(MOST, 2), bf16),
-            jax.ShapeDtypeStruct(tiles_of(16, 2, 4), bf16),
-            jax.ShapeDtypeStruct((2, 16, 128), i32),
-            jax.ShapeDtypeStruct((2, KT, 128), i32),
-            jax.ShapeDtypeStruct((8, 128), i32),
+            pltpu.VMEM(tiles_of(MOST, 2), bf16),
+            pltpu.VMEM(tiles_of(16, 2, 4), bf16),
+            pltpu.VMEM((2, 16, 128), i32),
+            pltpu.VMEM((2, KT, 128), i32),
+            pltpu.VMEM((8, 128), i32),
         ),
         in_specs=[SMEM, VMEM, VMEM, VMEM],
         out_specs=(VMEM,) * 5,
@@ -391,7 +412,7 @@
             pltpu.SemaphoreType.DMA((N_SEMS,)),
             pltpu.SemaphoreType.DMA((N_SEMS,)),
         ],
-        compiler_params=pltpu.CompilerParams(collective_id=0, has_side_effects=True, vmem_limit_bytes=48 << 20),
+        compiler_params=pltpu.CompilerParams(collective_id=0, has_side_effects=True, vmem_limit_bytes=30 << 20),
         name="exchange",
     )(sections, pa, pb, msg)
 
@@ -499,7 +520,7 @@
             jax.ShapeDtypeStruct((16, 16), jnp.int32),
         ),
         in_specs=[VMEM, VMEM, SMEM, SMEM, VMEM],
-        out_specs=(ANY, VMEM),
+        out_specs=(HBM, VMEM),
         scratch_shapes=[
             pltpu.VMEM((2048, 2048), jnp.bfloat16),
             pltpu.VMEM((256, 2048), jnp.bfloat16),
@@ -507,7 +528,7 @@
             pltpu.SMEM((16,), jnp.int32),
             pltpu.SemaphoreType.DMA((16,)),
         ],
-        compiler_params=pltpu.CompilerParams(vmem_limit_bytes=48 << 20),
+        compiler_params=pltpu.CompilerParams(vmem_limit_bytes=36 << 20),
         name="product",
     )(af, bf, afl, bfl, off)
 

time: 125 us -> 114 us (0.912); the launches traced: 125 us -> 113 us
  local copies, waits for them, and re-layouts: 11.9 us -> 1.36 us
  Pallas kernels: 113 us -> 111 us
    unnamed x15 -> x3, local copies, waits for them, and re-layouts: 11.9 us -> 1.36 us
    pallas_call x1, Pallas kernels: 39.5 us -> 37.2 us  [products(): pl.pallas_call(product_kernel, out_shape=(jax.ShapeDtypeStruct((2048, 204...]
where the time goes in v2:
time: 114 us; the launch traced here: 113 us
  Pallas kernels  111 us (97%)
  local copies, waits for them, and re-layouts  1.36 us (1%)
    pallas_call x1, Pallas kernels, exchanged(): pl.pallas_call(exchange_kernel, out_shape=(pltpu.VMEM(tiles_of(MOST, 2),...  65.3 us
    pallas_call x1, Pallas kernels, products(): pl.pallas_call(product_kernel, out_shape=(jax.ShapeDtypeStruct((2048, 204...  37.2 us
    pallas_call x1, Pallas kernels, packed_panels(): pl.pallas_call(pack_kernel, out_shape=(pltpu.VMEM(tiles_of(MOST), jnp.bfl...  8.44 us

profile of v2, /device:TPU:1, one launch (start us, length us, event | category | flops | bytes accessed | tf_op | source)
XLA Modules:
  0.0 112.9 jit_solution(17267274906798582117)
XLA Ops:
  0.6 1.4 %copy.7.af_h = s32[16,8]{1,0:T(8,128)} copy(s32[16,8]{0,1:T(8,128)} %param.6) | data formatting | bytes 1024 | tf_op args[1]
  2.0 0.0 copy-start
  2.0 8.4 %pack.1 = (bf16[64,128,128]{2,1,0:T(8,128)(2,1)S(1)}, bf16[2,64,128,128]{3,2,1,0:T(8,128)(2,1)S(1)}, s32[16,128]{1,0:T(8,128)S(1)}) custom-call(s32[2]{0:T(128)} %sec.1, s32[16,8]{1,0:T(8,128)} %copy.7.af_h, s32[16,16]{1,0:T(8,128)} %bf_h.1, bf16[2048,1024]{1,0:T(8,128)(2,1)} %a_hbm.1, bf16[2048,2048]{1,0:T(8,128)(2,1)} %b_hbm.1), custom_call_target="tpu_custom_call" | custom-call | tf_op jit(solution)/shard_map/pack/pallas_call | solution.py:87
  10.4 0.0 copy-done
  10.4 65.3 %exchange.1 = (bf16[64,2,128,128]{3,2,1,0:T(8,128)(2,1)S(1)}, bf16[16,2,4,128,128]{4,3,2,1,0:T(8,128)(2,1)S(1)}, s32[2,16,128]{2,1,0:T(8,128)S(1)}, s32[2,8,128]{2,1,0:T(8,128)S(1)}, s32[8,128]{1,0:T(8,128)S(1)}) custom-call(s32[2]{0:T(128)S(1)} %copy-done, bf16[64,128,128]{2,1,0:T(8,128)(2,1)S(1)} %get-tuple-element.10.pa, ...), custom_call_target="tpu_custom_call" | custom-call | tf_op jit(solution)/shard_map/exchange/pallas_call | solution.py:381
  75.7 37.2 %product.1 = (bf16[2048,2048]{1,0:T(8,128)(2,1)}, s32[16,16]{1,0:T(8,128)}) custom-call(bf16[64,2,128,128]{3,2,1,0:T(8,128)(2,1)S(1)} %get-tuple-element.13.af, bf16[16,2,4,128,128]{4,3,2,1,0:T(8,128)(2,1)S(1)} %get-tuple-element.14.bf, s32[2,16,128]{2,1,0:T(8,128)S(1)} %get-tuple-element.15.afl, s32[2,8,128]{2,1,0:T(8,128)S(1)} %get-tuple-element.16.bfl, ...), custom_call_target="tpu_custom_call" | custom-call | tf_op jit(solution)/shard_map/product/pallas_call | solution.py:516
Async XLA Ops:
  2.0 8.4 %copy-start = (s32[2]{0:T(128)S(1)}, s32[2]{0:T(128)}, u32[]{:S(2)}) copy-start(s32[2]{0:T(128)} %sec.1) | copy-start | bytes 28
